TPU v7x, 32 devices: a whole 2x2x4 slice. The times are simulated.
32 devices in a mesh: dp: 8 (over z, y), seq: 4 (over x, core).
Axes of the slice: x: 2, y: 2, z: 4, core: 2. Of those that a mesh axis runs over, the one named last changes fastest.
Arguments:
- inputs: bfloat16 [48, 1024, 256], P('dp', 'seq')
- cotangent: bfloat16 [48, 1024, 256], P('dp', 'seq')
- owner_list: int32 [7], replicated, may hold values from 0 to 7, as said below
- master_rows: float32 [8, 524288], P('dp'), as said below
- moment1_rows: float32 [8, 524288], P('dp'), as said below
- moment2_rows: float32 [8, 524288], P('dp'), as said below
Outputs:
- final_state: float32 [48, 1024, 256], P('dp', 'seq')
- input_grad: float32 [48, 1024, 256], P('dp', 'seq')
- state_stats: float32 [2, 48], replicated
- new_moment1: float32 [8, 524288], P('dp')
- new_moment2: float32 [8, 524288], P('dp')
- new_master: float32 [8, 524288], P('dp')
Inputs may be any that keep to these rules, and one draw needn't show every extreme that they name: Tensor t goes to dp index owner_list[t]. W_up and W_down share one owner that holds no other tensor, so the busiest owner holds 524288 entries; the other five tensors are dealt among the other indices, several may share one. `master_rows`: entries of a row beyond the tensors its owner holds are not read. `moment1_rows`: entries of a row beyond the tensors its owner holds are not read. `moment2_rows`: Positive. Entries beyond the tensors an owner holds are not read.
All inputs are finite; a program needn't handle non-finite values.
Results may differ from a plain program's by a relative error of at most 0.02.
The roundings to bfloat16 on the way count: a program that leaves them out, or rounds other values in their place, can miss the bound.
Values may be sent and summed in bfloat16 or wider, within the bound.
A program may use at most 192 MiB of HBM per device.

v0:
```python
from functools import partial
import jax
import jax.numpy as jnp
from jax import lax
from jax.sharding import PartitionSpec as P

D = 256
HEADS = 4
HD = 64
FF = 1024
STEP = 3
SMALL = 9
norm_eps = 1e-05
stat_eps = 1e-06
adam_eps = 1e-08
masked_score = -1e30


def tensor_shapes():
    return [(D, D), (D, D), (D, D), (D, D), (D, FF), (FF, D), (SMALL, D)]


def owner_starts(owner_list):
    shapes = tensor_shapes()
    starts = []
    for tensor_id in range(7):
        offset = jnp.zeros((), jnp.int32)
        for earlier in range(tensor_id):
            shared = (owner_list[earlier] == owner_list[tensor_id]).astype(jnp.int32)
            offset = offset + shared * (shapes[earlier][0] * shapes[earlier][1])
        starts.append(offset)
    return starts


def layer_norm(values, norm_gain, norm_shift):
    average = jnp.mean(values, axis=-1, keepdims=True)
    centered = values - average
    spread = jnp.mean(centered * centered, axis=-1, keepdims=True)
    return centered * lax.rsqrt(spread + norm_eps) * norm_gain + norm_shift


def masked_scores(packed):
    length = packed.shape[0]
    queries = packed[:, :, :HD]
    keys_part = packed[:, :, HD : 2 * HD]
    scores = jnp.einsum(
        "qhd,khd->hqk", queries, keys_part, preferred_element_type=jnp.float32
    ) * HD ** (-0.5)
    causal = lax.broadcasted_iota(jnp.int32, (length, length), 0) >= lax.broadcasted_iota(
        jnp.int32, (length, length), 1
    )
    return jnp.where(causal[None], scores, masked_score)


def attend_single(packed):
    scores = masked_scores(packed)
    highest_score = jnp.max(scores, axis=-1, keepdims=True)
    raw_weights = jnp.exp(scores - highest_score)
    totals = jnp.sum(raw_weights, axis=-1, keepdims=True)
    attention_probs = raw_weights / totals
    values_part = packed[:, :, 2 * HD :]
    attention_output = jnp.einsum(
        "hqk,khd->qhd",
        attention_probs.astype(jnp.bfloat16),
        values_part,
        preferred_element_type=jnp.float32,
    )
    return (attention_output.astype(jnp.bfloat16), (highest_score + jnp.log(totals))[..., 0])


def attend_items(packed_items):
    attention_output, log_total = lax.map(attend_single, packed_items)
    return (attention_output, log_total, packed_items)


def attend_single_back(parts):
    packed, log_total, grad_attended = parts
    queries = packed[:, :, :HD]
    keys_part = packed[:, :, HD : 2 * HD]
    values_part = packed[:, :, 2 * HD :]
    scores = masked_scores(packed)
    attention_probs = jnp.exp(scores - log_total[..., None])
    grad_probs = jnp.einsum(
        "qhd,khd->hqk", grad_attended, values_part, preferred_element_type=jnp.float32
    )
    inner_sum = jnp.sum(attention_probs * grad_probs, axis=-1, keepdims=True)
    grad_scores = (attention_probs * (grad_probs - inner_sum)).astype(jnp.bfloat16)
    grad_queries = jnp.einsum(
        "hqk,khd->qhd", grad_scores, keys_part, preferred_element_type=jnp.float32
    ) * HD ** (-0.5)
    grad_keys = jnp.einsum(
        "hqk,qhd->khd", grad_scores, queries, preferred_element_type=jnp.float32
    ) * HD ** (-0.5)
    grad_values = jnp.einsum(
        "hqk,qhd->khd",
        attention_probs.astype(jnp.bfloat16),
        grad_attended,
        preferred_element_type=jnp.float32,
    )
    return jnp.concatenate([grad_queries, grad_keys, grad_values], axis=-1).astype(jnp.bfloat16)


def block_forward(loop_state, combined_weight, output_weight, up_weight, down_weight, small_piece):
    seq_count, quarter, features = loop_state.shape
    normalized_input = layer_norm(loop_state, small_piece[0], small_piece[1]).astype(jnp.bfloat16)
    projected = jnp.einsum(
        "fur,rk->fuk", normalized_input, combined_weight, preferred_element_type=jnp.float32
    ).astype(jnp.bfloat16)
    per_head = projected.reshape(seq_count, quarter, HEADS, 3 * HD)
    head_out, log_total, packed = attend_items(
        lax.all_to_all(per_head, "seq", split_axis=2, concat_axis=1, tiled=True)
    )
    attention_output = lax.all_to_all(
        head_out, "seq", split_axis=1, concat_axis=2, tiled=True
    ).reshape(seq_count, quarter, features)
    middle_state = loop_state + jnp.einsum(
        "fur,rk->fuk", attention_output, output_weight, preferred_element_type=jnp.float32
    )
    normalized_middle = layer_norm(middle_state, small_piece[2], small_piece[3]).astype(
        jnp.bfloat16
    )
    before = jnp.einsum(
        "sgm,mk->sgk", normalized_middle, up_weight, preferred_element_type=jnp.float32
    ) + small_piece[5:].reshape(FF)
    hidden_units = jax.nn.gelu(before, approximate=False).astype(jnp.bfloat16)
    result = middle_state + (
        jnp.einsum("czm,mg->czg", hidden_units, down_weight, preferred_element_type=jnp.float32)
        + small_piece[4]
    )
    saved = (
        loop_state,
        normalized_input,
        packed,
        log_total,
        attention_output,
        middle_state,
        normalized_middle,
        before,
        hidden_units,
    )
    return (result, saved)


def block_backward(
    grad_result, saved, combined_weight, output_weight, up_weight, down_weight, small_piece
):
    (
        loop_state,
        normalized_input,
        packed,
        log_total,
        attention_output,
        middle_state,
        normalized_middle,
        before,
        hidden_units,
    ) = saved
    seq_count, quarter, features = loop_state.shape
    branch_gradient = grad_result.astype(jnp.bfloat16)
    down_gradient = jnp.einsum(
        "yeo,yen->on", hidden_units, branch_gradient, preferred_element_type=jnp.float32
    )
    grad_bias_down = jnp.sum(branch_gradient.astype(jnp.float32), axis=(0, 1))
    hidden_gradient = jnp.einsum(
        "vel,kl->vek", branch_gradient, down_weight, preferred_element_type=jnp.float32
    )
    gelu_pull = jax.vjp(partial(jax.nn.gelu, approximate=False), before)[1]
    gradient_prior = gelu_pull(hidden_gradient)[0].astype(jnp.bfloat16)
    up_gradient = jnp.einsum(
        "erv,erh->vh", normalized_middle, gradient_prior, preferred_element_type=jnp.float32
    )
    grad_bias_up = jnp.sum(gradient_prior.astype(jnp.float32), axis=(0, 1))
    grad_normed_mid = jnp.einsum(
        "tam,em->tae", gradient_prior, up_weight, preferred_element_type=jnp.float32
    )
    second_pull = jax.vjp(layer_norm, middle_state, small_piece[2], small_piece[3])[1]
    grad_mid_part, grad_gain_two, grad_shift_two = second_pull(grad_normed_mid)
    grad_middle = grad_result + grad_mid_part
    attention_gradient = grad_middle.astype(jnp.bfloat16)
    grad_out_weight = jnp.einsum(
        "tck,tcp->kp", attention_output, attention_gradient, preferred_element_type=jnp.float32
    )
    grad_attended = jnp.einsum(
        "tkh,nh->tkn", attention_gradient, output_weight, preferred_element_type=jnp.float32
    ).astype(jnp.bfloat16)
    grad_heads = lax.all_to_all(
        grad_attended.reshape(seq_count, quarter, HEADS, HD),
        "seq",
        split_axis=2,
        concat_axis=1,
        tiled=True,
    )
    grad_packed = lax.map(attend_single_back, (packed, log_total, grad_heads))
    projected_gradient = lax.all_to_all(
        grad_packed, "seq", split_axis=1, concat_axis=2, tiled=True
    ).reshape(seq_count, quarter, 3 * features)
    grad_joined = jnp.einsum(
        "tck,tcp->kp", normalized_input, projected_gradient, preferred_element_type=jnp.float32
    )
    grad_normed = jnp.einsum(
        "tkh,nh->tkn", projected_gradient, combined_weight, preferred_element_type=jnp.float32
    )
    first_pull = jax.vjp(layer_norm, loop_state, small_piece[0], small_piece[1])[1]
    grad_state_part, grad_gain_one, grad_shift_one = first_pull(grad_normed)
    grad_state = grad_middle + grad_state_part
    grad_small = jnp.concatenate(
        [
            jnp.stack(
                [grad_gain_one, grad_shift_one, grad_gain_two, grad_shift_two, grad_bias_down]
            ),
            grad_bias_up.reshape(FF // D, D),
        ],
        axis=0,
    )
    return (grad_state, (grad_joined, grad_out_weight, up_gradient, down_gradient, grad_small))


def gather_stat(square_sums):
    return lax.all_gather(square_sums, ("dp", "seq"), axis=1, tiled=True)


def finish_stats(gathered, entries_total):
    loop_count = gathered.shape[0]
    folded = gathered.reshape(loop_count, lax.axis_size("dp"), lax.axis_size("seq"), -1)
    folded = jnp.sum(folded, axis=2).reshape(loop_count, -1)
    return jnp.sqrt(folded / entries_total + stat_eps)


def split_joined(grad_joined):
    arranged = grad_joined.reshape(D, HEADS, 3, HD)
    return [arranged[:, :, slot_id, :].reshape(D, D) for slot_id in range(3)]


def per_device(inputs, cotangent, owner_list, master_rows, moment1_rows, moment2_rows):
    shapes = tensor_shapes()
    starts = owner_starts(owner_list)
    device_row = lax.axis_index("dp")
    zero_row = jnp.zeros((), jnp.int32)
    owned_parts = []
    for tensor_id in range(7):
        entries = shapes[tensor_id][0] * shapes[tensor_id][1]
        sliced = lax.dynamic_slice(
            master_rows, (zero_row, starts[tensor_id]), (1, entries)
        ).reshape(shapes[tensor_id])
        is_owner = owner_list[tensor_id] == device_row
        owned_parts.append(jnp.where(is_owner, sliced, 0.0))
    masters = lax.psum(
        (
            owned_parts[0],
            owned_parts[1],
            owned_parts[2],
            owned_parts[3],
            owned_parts[4],
            owned_parts[5],
            owned_parts[6],
        ),
        "dp",
    )
    small_piece = masters[6]
    matrices = [matrix.astype(jnp.bfloat16) for matrix in masters[:6]]
    query_low, key_low, value_low, out_low, up_low, down_low = matrices
    combined_weight = jnp.stack(
        [
            query_low.reshape(D, HEADS, HD),
            key_low.reshape(D, HEADS, HD),
            value_low.reshape(D, HEADS, HD),
        ],
        axis=2,
    ).reshape(D, 3 * D)
    start_state = inputs.astype(jnp.float32)
    seq_count, quarter, features = start_state.shape
    entries_total = quarter * lax.axis_size("seq") * features
    first_out, first_saved = block_forward(
        start_state, combined_weight, out_low, up_low, down_low, small_piece
    )
    first_squares = jnp.sum(first_out * first_out, axis=(1, 2))
    first_gathered = gather_stat(first_squares[None])
    second_out, second_saved = block_forward(
        first_out + start_state, combined_weight, out_low, up_low, down_low, small_piece
    )
    second_squares = jnp.sum(second_out * second_out, axis=(1, 2))
    second_gathered = gather_stat(second_squares[None])
    gathered = jnp.concatenate([first_gathered, second_gathered], axis=0)
    state_stats = finish_stats(gathered, entries_total)
    grad_second_in, grads_two = block_backward(
        cotangent.astype(jnp.float32),
        second_saved,
        combined_weight,
        out_low,
        up_low,
        down_low,
        small_piece,
    )
    grad_first_in, grads_one = block_backward(
        grad_second_in, first_saved, combined_weight, out_low, up_low, down_low, small_piece
    )
    local_sums = [part_two + part_one for part_two, part_one in zip(grads_two, grads_one)]
    summed = lax.psum(
        (local_sums[0], local_sums[1], local_sums[2], local_sums[3], local_sums[4]), ("dp", "seq")
    )
    input_grad = grad_second_in + grad_first_in
    gradients = split_joined(summed[0]) + [summed[1], summed[2], summed[3], summed[4]]
    learning_rates = [D ** (-0.5)] * 5 + [FF ** (-0.5), 0.5]
    decays_list = [0.1] * 6 + [0.0]
    correction = 1.0 - 0.5**STEP
    new_moment1 = jnp.zeros_like(moment1_rows)
    new_moment2 = jnp.zeros_like(moment2_rows)
    new_master = jnp.zeros_like(master_rows)
    for tensor_id in range(7):
        entries = shapes[tensor_id][0] * shapes[tensor_id][1]
        corner = (zero_row, starts[tensor_id])
        is_owner = owner_list[tensor_id] == device_row
        gradient = gradients[tensor_id].reshape(1, entries)
        old_first = lax.dynamic_slice(moment1_rows, corner, (1, entries))
        old_second = lax.dynamic_slice(moment2_rows, corner, (1, entries))
        old_weight = lax.dynamic_slice(master_rows, corner, (1, entries))
        first_new = 0.5 * old_first + 0.5 * gradient
        second_new = 0.5 * old_second + 0.5 * gradient * gradient
        update = (
            first_new / correction / (jnp.sqrt(second_new / correction) + adam_eps)
            + decays_list[tensor_id] * old_weight
        )
        weight_new = old_weight - learning_rates[tensor_id] * update
        new_moment1 = lax.dynamic_update_slice(
            new_moment1,
            jnp.where(is_owner, first_new, lax.dynamic_slice(new_moment1, corner, (1, entries))),
            corner,
        )
        new_moment2 = lax.dynamic_update_slice(
            new_moment2,
            jnp.where(is_owner, second_new, lax.dynamic_slice(new_moment2, corner, (1, entries))),
            corner,
        )
        new_master = lax.dynamic_update_slice(
            new_master,
            jnp.where(is_owner, weight_new, lax.dynamic_slice(new_master, corner, (1, entries))),
            corner,
        )
    return (second_out, input_grad, state_stats, new_moment1, new_moment2, new_master)


def solution(mesh):
    placed = (
        P("dp", "seq", None),
        P("dp", "seq", None),
        P(),
        P("dp", None),
        P("dp", None),
        P("dp", None),
    )
    return jax.shard_map(
        per_device,
        mesh=mesh,
        in_specs=placed,
        out_specs=(
            P("dp", "seq", None),
            P("dp", "seq", None),
            P(),
            P("dp", None),
            P("dp", None),
            P("dp", None),
        ),
        check_vma=False,
    )
```

profile of v0, /device:TPU:0, one launch (start us, length us, event | category | flops | bytes accessed | tf_op | source)
XLA Modules:
  0.0 949.5 jit_solution(13561079497772902134)
XLA Ops:
  40.8 13.1 %fusion.104 = (f32[262144]{0:T(1024)S(1)}, f32[262144]{0:T(1024)}) fusion(pred[]{:T(512)S(6)} %eq.113, f32[1,524288]{1,0:T(1,128)} %param.17, s32[]{:T(128)S(6)} %select_n.271, s32[]{:T(128)S(6)} %select_n.267, pred[]{:T(512)S(6)} %eq.108), kind=kLoop, calls=%fused_computation.227 | loop fusion | flops 524288 | bytes 4194314 | tf_op jit(solution)/shard_map/jit(_where)/select_n | solution.py:246
  69.9 132.7 %all-reduce.12 = (bf16[256,256]{1,0:T(8,128)(2,1)S(1)}, bf16[256,256]{1,0:T(8,128)(2,1)S(1)}, bf16[256,256]{1,0:T(8,128)(2,1)S(1)}, f32[9,256]{1,0:T(8,128)S(1)}...) all-reduce(f32[256,256]{1,0:T(8,128)} %select_n.261, ...), channel_id=1, replica_groups=mesh['dp'=8,'seq'=4] {'dp'}, use_global_device_ids=true, to_apply=%region_5.6 | all-reduce | flops 788736 | bytes 4737024 | tf_op jit(solution)/shard_map/psum | solution.py:247
  218.2 28.5 %all-to-all-done = bf16[6,256,4,192]{1,3,0,2:T(8,128)(2,1)} async-done(((bf16[6,256,4,192]{1,3,0,2:T(8,128)(2,1)}), bf16[6,256,4,192]{1,3,0,2:T(8,128)(2,1)}, u32[]{:S(2)}, u32[]{:S(2)}) %all-to-all-start) | async-done | bytes 2359328 | tf_op jit(solution)/shard_map/all_to_all | solution.py:111
  250.2 18.3 %while.44 = (s32[]{:T(128)}, bf16[6,1024,1,64]{1,3,2,0:T(8,128)(2,1)S(1)}, f32[6,1,1024]{2,1,0:T(1,128)S(1)}, bf16[6,1024,1,192]{1,3,2,0:T(8,128)(2,1)}, s32[]{:T(128)}) while((s32[]{:T(128)}, bf16[6,1024,1,64]{1,3,2,0:T(8,128)(2,1)S(1)}, f32[6,1,1024]{2,1,0:T(1,128)S(1)}, bf16[6,1024,1,192]{1,3,2,0:T(8,128)(2,1)}, s32[]{:T(128)}) %tuple.165), condition=%wide.region_9.10_spmd, body=%wide.region_6.9_spmd.sunk | while | flops 284228608 | bytes 13934665 | solution.py:72
  279.2 11.5 %all-to-all-done.1 = bf16[4,2,49152]{2,1,0:T(2,128)(2,1)S(1)} async-done(((bf16[4,2,49152]{2,1,0:T(2,128)(2,1)}), bf16[4,2,49152]{2,1,0:T(2,128)(2,1)S(1)}, u32[]{:S(2)}, u32[]{:S(2)}) %all-to-all-start.1) | async-done | bytes 786464 | tf_op jit(solution)/shard_map/all_to_all | solution.py:113
  300.9 15.2 %multiply_convert_fusion.3 = (bf16[6,256,1024]{2,1,0:T(8,128)(2,1)S(1)}, f32[6,256,1024]{2,1,0:T(8,128)}) fusion(f32[6,256,1024]{2,1,0:T(8,128)S(1)} %get-tuple-element.342, f32[1024]{0:T(1024)S(1)} %bitcast.501, u8[256,1024]{1,0:T(8,128)(4,1)S(1)} %get-tuple-element.217, u8[256,1024]{1,0:T(8,128)(4,1)S(1)} %get-tuple-element.216), kind=kLoop, calls=%fused_computation.130 | loop fusion | flops 111673344 | bytes 16257024 | tf_op jit(solution)/shard_map/convert_element_type | solution.py:125
  332.9 28.5 %all-to-all-done.2 = bf16[6,256,4,192]{1,3,0,2:T(8,128)(2,1)} async-done(((bf16[6,256,4,192]{1,3,0,2:T(8,128)(2,1)}), bf16[6,256,4,192]{1,3,0,2:T(8,128)(2,1)}, u32[]{:S(2)}, u32[]{:S(2)}) %all-to-all-start.2) | async-done | bytes 2359328 | tf_op jit(solution)/shard_map/all_to_all | solution.py:111
  364.9 18.3 %while.45 = (s32[]{:T(128)}, bf16[6,1024,1,64]{1,3,2,0:T(8,128)(2,1)S(1)}, f32[6,1,1024]{2,1,0:T(1,128)S(1)}, bf16[6,1024,1,192]{1,3,2,0:T(8,128)(2,1)}, s32[]{:T(128)}) while((s32[]{:T(128)}, bf16[6,1024,1,64]{1,3,2,0:T(8,128)(2,1)S(1)}, f32[6,1,1024]{2,1,0:T(1,128)S(1)}, bf16[6,1024,1,192]{1,3,2,0:T(8,128)(2,1)}, s32[]{:T(128)}) %tuple.167), condition=%wide.region_20.21_spmd, body=%wide.region_17.20_spmd.sunk | while | flops 284228608 | bytes 13934665 | solution.py:72
  394.9 10.4 %all-to-all-done.3 = bf16[4,2,49152]{2,1,0:T(2,128)(2,1)S(1)} async-done(((bf16[4,2,49152]{2,1,0:T(2,128)(2,1)}), bf16[4,2,49152]{2,1,0:T(2,128)(2,1)S(1)}, u32[]{:S(2)}, u32[]{:S(2)}) %all-to-all-start.3) | async-done | bytes 786464 | tf_op jit(solution)/shard_map/all_to_all | solution.py:113
  415.5 15.1 %multiply_convert_fusion.2 = (bf16[6,256,1024]{2,1,0:T(8,128)(2,1)}, f32[6,256,1024]{2,1,0:T(8,128)S(1)}) fusion(f32[6,256,1024]{2,1,0:T(8,128)S(1)} %get-tuple-element.345, f32[1024]{0:T(1024)S(1)} %bitcast.503, u8[256,1024]{1,0:T(8,128)(4,1)S(1)} %get-tuple-element.215, u8[256,1024]{1,0:T(8,128)(4,1)S(1)} %get-tuple-element.214), kind=kLoop, calls=%fused_computation.117 | loop fusion | flops 111673344 | bytes 16257024 | tf_op jit(solution)/shard_map/convert_element_type | solution.py:125
  448.9 11.7 %all-to-all-done.4 = bf16[6,256,4,64]{1,3,0,2:T(8,128)(2,1)} async-done(((bf16[6,256,4,64]{1,3,0,2:T(8,128)(2,1)}), bf16[6,256,4,64]{1,3,0,2:T(8,128)(2,1)}, u32[]{:S(2)}, u32[]{:S(2)}) %all-to-all-start.4) | async-done | bytes 786464 | tf_op jit(solution)/shard_map/all_to_all | solution.py:186
  464.3 52.6 %while.46 = (s32[]{:T(128)}, bf16[6,1024,1,192]{1,3,2,0:T(8,128)(2,1)}, bf16[6,1024,1,192]{1,3,2,0:T(8,128)(2,1)}, f32[6,1,1024]{2,1,0:T(1,128)S(1)}, bf16[6,1024,1,64]{1,3,2,0:T(8,128)(2,1)}, /*index=5*/s32[]{:T(128)}) while((s32[]{:T(128)}, bf16[6,1024,1,192]{1,3,2,0:T(8,128)(2,1)}, bf16[6,1024,1,192]{1,3,2,0:T(8,128)(2,1)}, ...), condition=%wide.region_27.28_spmd, body=%wide.region_25.27_spmd.sunk | while | flops 683080704 | bytes 34362956 | solution.py:193
  516.9 6.6 copy.295
  523.5 53.8 %all_to_all.132 = bf16[6,1024,1,192]{3,0,2,1:T(8,128)(2,1)} all-to-all(bf16[6,1024,1,192]{3,0,2,1:T(8,128)(2,1)} %copy.295), channel_id=1, replica_groups=mesh['dp'=8,'seq'=4] {'seq'}, dimensions={1} | all-to-all | bytes 4718592 | tf_op jit(solution)/shard_map/all_to_all | solution.py:194
  577.3 5.6 copy.368
  594.6 7.0 convert_reduce_fusion
  633.3 56.6 %while.47 = (s32[]{:T(128)}, bf16[6,1024,1,192]{1,3,2,0:T(8,128)(2,1)}, bf16[6,1024,1,192]{1,3,2,0:T(8,128)(2,1)}, f32[6,1,1024]{2,1,0:T(1,128)}, bf16[6,1024,1,64]{1,3,2,0:T(8,128)(2,1)}, /*index=5*/s32[]{:T(128)}) while((s32[]{:T(128)}, bf16[6,1024,1,192]{1,3,2,0:T(8,128)(2,1)}, bf16[6,1024,1,192]{1,3,2,0:T(8,128)(2,1)}, ...), condition=%wide.region_34.35_spmd, body=%wide.region_32.34_spmd.sunk | while | flops 683080704 | bytes 34362956 | solution.py:193
  689.9 6.5 copy.310
  715.5 34.0 %all-to-all-done.7 = bf16[6,1024,1,192]{3,0,2,1:T(8,128)(2,1)} async-done(((bf16[6,1024,1,192]{3,0,2,1:T(8,128)(2,1)}), bf16[6,1024,1,192]{3,0,2,1:T(8,128)(2,1)}, u32[]{:S(2)}, u32[]{:S(2)}) %all-to-all-start.7) | async-done | bytes 2359328 | tf_op jit(solution)/shard_map/all_to_all | solution.py:194
  749.5 5.6 copy.372
  765.9 39.1 %all-reduce.5 = (f32[192]{0:T(256)S(1)}, f32[192]{0:T(256)S(1)}, f32[1,2304]{1,0:T(1,128)S(1)}) all-reduce(f32[192]{0:T(256)S(1)} %dynamic-update-slice.1, f32[192]{0:T(256)S(1)} %dynamic-update-slice, f32[1,2304]{1,0:T(1,128)S(1)} %bitcast.506), channel_id=3, replica_groups=mesh['dp'=8,'seq'=4] {'dp','seq'}, use_global_device_ids=true, to_apply=%add.4 | all-reduce | flops 2688 | bytes 21504
  812.7 88.7 %all-reduce.11.cloned.1.call-done = (f32[256,4,3,64]{0,3,2,1:T(8,128)}, f32[1,65536]{1,0:T(1,128)}, f32[1,262144]{1,0:T(1,128)}, f32[1,262144]{1,0:T(1,128)}) async-done(((f32[256,4,3,64]{0,3,2,1:T(8,128)}, f32[1,65536]{1,0:T(1,128)}, f32[1,262144]{1,0:T(1,128)}, f32[1,262144]{1,0:T(1,128)}), (f32[256,4,3,64]{0,3,2,1:T(8,128)}, f32[1,65536]{1,0:T(1,128)}, f32[1,262144]{1,0:T(1,128)}, ...) | async-done | bytes 3145744 | tf_op jit(solution)/shard_map/psum | solution.py:298
  925.2 7.1 fusion.103
  932.3 7.1 fusion.107
  (493 shorter events, 372.7 us)
Async XLA Ops:
  69.9 133.1 %copy-start.42 = (bf16[6,256,256]{2,1,0:T(8,128)(2,1)S(1)}, bf16[6,256,256]{2,1,0:T(8,128)(2,1)}, u32[]{:S(2)}) copy-start(bf16[6,256,256]{2,1,0:T(8,128)(2,1)} %param.14) | copy-start | bytes 2359300
  203.0 115.3 %copy-start.35 = (bf16[256,4,3,64]{0,3,2,1:T(8,128)(2,1)}, bf16[256,4,3,64]{0,3,2,1:T(8,128)(2,1)S(1)}, u32[]{:S(2)}) copy-start(bf16[256,4,3,64]{0,3,2,1:T(8,128)(2,1)S(1)} %copy.259) | copy-start | bytes 1179652
  203.0 113.1 %copy-start.63 = (f32[1,256]{1,0:T(1,128)}, f32[1,256]{1,0:T(1,128)S(1)}, u32[]{:S(2)}) copy-start(f32[1,256]{1,0:T(1,128)S(1)} %get-tuple-element.328) | copy-start | bytes 3076
  203.0 115.3 %copy-start.65 = (f32[1,256]{1,0:T(1,128)}, f32[1,256]{1,0:T(1,128)S(1)}, u32[]{:S(2)}) copy-start(f32[1,256]{1,0:T(1,128)S(1)} %get-tuple-element.331) | copy-start | bytes 3076
  203.1 209.1 %copy-start.67 = (f32[1,256]{1,0:T(1,128)}, f32[1,256]{1,0:T(1,128)S(1)}, u32[]{:S(2)}) copy-start(f32[1,256]{1,0:T(1,128)S(1)} %get-tuple-element.329) | copy-start | bytes 3076
  203.3 112.8 %copy-start = (bf16[6,256,256]{1,2,0:T(8,128)(2,1)}, bf16[6,256,256]{1,2,0:T(8,128)(2,1)S(1)}, u32[]{:S(2)}) copy-start(bf16[6,256,256]{1,2,0:T(8,128)(2,1)S(1)} %copy.255) | copy-start | bytes 2359300
  213.7 33.0 %all-to-all-start = ((bf16[6,256,4,192]{1,3,0,2:T(8,128)(2,1)}), bf16[6,256,4,192]{1,3,0,2:T(8,128)(2,1)}, u32[]{:S(2)}, u32[]{:S(2)}) async-start(bf16[6,256,4,192]{1,3,0,2:T(8,128)(2,1)} %copy.263), calls=%async_computation | async-start | bytes 4718592 | tf_op jit(solution)/shard_map/all_to_all | solution.py:111
  275.2 15.5 %all-to-all-start.1 = ((bf16[4,2,49152]{2,1,0:T(2,128)(2,1)}), bf16[4,2,49152]{2,1,0:T(2,128)(2,1)S(1)}, u32[]{:S(2)}, u32[]{:S(2)}) async-start(bf16[4,2,49152]{2,1,0:T(2,128)(2,1)} %reshape.839), calls=%async_computation.1 | async-start | bytes 1572864 | tf_op jit(solution)/shard_map/all_to_all | solution.py:113
  297.3 18.9 %copy-start.3 = (f32[6,256,256]{1,2,0:T(8,128)}, f32[6,256,256]{1,2,0:T(8,128)S(1)}, u32[]{:S(2)}) copy-start(f32[6,256,256]{1,2,0:T(8,128)S(1)} %get-tuple-element.341) | copy-start | bytes 4718596
  300.9 15.3 %copy-start.29 = (f32[6,256,1024]{2,1,0:T(8,128)}, f32[6,256,1024]{2,1,0:T(8,128)S(1)}, u32[]{:S(2)}) copy-start(f32[6,256,1024]{2,1,0:T(8,128)S(1)} %get-tuple-element.342) | copy-start | bytes 18874372
  300.9 15.3 %copy-start.46 = (bf16[1024,256]{0,1:T(8,128)(2,1)S(1)}, bf16[1024,256]{0,1:T(8,128)(2,1)}, u32[]{:S(2)}) copy-start(bf16[1024,256]{0,1:T(8,128)(2,1)} %get-tuple-element.281) | copy-start | bytes 1572868
  328.4 33.0 %all-to-all-start.2 = ((bf16[6,256,4,192]{1,3,0,2:T(8,128)(2,1)}), bf16[6,256,4,192]{1,3,0,2:T(8,128)(2,1)}, u32[]{:S(2)}, u32[]{:S(2)}) async-start(bf16[6,256,4,192]{1,3,0,2:T(8,128)(2,1)} %copy.276), calls=%async_computation.2 | async-start | bytes 4718592 | tf_op jit(solution)/shard_map/all_to_all | solution.py:111
  385.8 8.0 copy-start.43
  390.1 15.2 %all-to-all-start.3 = ((bf16[4,2,49152]{2,1,0:T(2,128)(2,1)}), bf16[4,2,49152]{2,1,0:T(2,128)(2,1)S(1)}, u32[]{:S(2)}, u32[]{:S(2)}) async-start(bf16[4,2,49152]{2,1,0:T(2,128)(2,1)} %reshape.841), calls=%async_computation.3 | async-start | bytes 1572864 | tf_op jit(solution)/shard_map/all_to_all | solution.py:113
  415.5 15.1 %copy-start.44 = (bf16[6,256,256]{2,1,0:T(8,128)(2,1)S(1)}, bf16[6,256,256]{2,1,0:T(8,128)(2,1)}, u32[]{:S(2)}) copy-start(bf16[6,256,256]{2,1,0:T(8,128)(2,1)} %param.15) | copy-start | bytes 2359300
  415.5 15.1 %copy-start.47 = (bf16[1024,256]{0,1:T(8,128)(2,1)S(1)}, bf16[1024,256]{0,1:T(8,128)(2,1)}, u32[]{:S(2)}) copy-start(bf16[1024,256]{0,1:T(8,128)(2,1)} %get-tuple-element.281) | copy-start | bytes 1572868
  444.4 16.1 %all-to-all-start.4 = ((bf16[6,256,4,64]{1,3,0,2:T(8,128)(2,1)}), bf16[6,256,4,64]{1,3,0,2:T(8,128)(2,1)}, u32[]{:S(2)}, u32[]{:S(2)}) async-start(bf16[6,256,4,64]{1,3,0,2:T(8,128)(2,1)} %copy.291), calls=%async_computation.4 | async-start | bytes 1572864 | tf_op jit(solution)/shard_map/all_to_all | solution.py:186
  613.3 16.3 %all-to-all-start.6 = ((bf16[6,256,4,64]{1,3,0,2:T(8,128)(2,1)}), bf16[6,256,4,64]{1,3,0,2:T(8,128)(2,1)}, u32[]{:S(2)}, u32[]{:S(2)}) async-start(bf16[6,256,4,64]{1,3,0,2:T(8,128)(2,1)} %copy.306), calls=%async_computation.6 | async-start | bytes 1572864 | tf_op jit(solution)/shard_map/all_to_all | solution.py:186
  696.4 53.1 %all-to-all-start.7 = ((bf16[6,1024,1,192]{3,0,2,1:T(8,128)(2,1)}), bf16[6,1024,1,192]{3,0,2,1:T(8,128)(2,1)}, u32[]{:S(2)}, u32[]{:S(2)}) async-start(bf16[6,1024,1,192]{3,0,2,1:T(8,128)(2,1)} %copy.310), calls=%async_computation.7 | async-start | bytes 8388608 | tf_op jit(solution)/shard_map/all_to_all | solution.py:194
  701.3 200.0 %all-reduce.11.cloned.1.call-start = ((), (), s32[]{:S(2)}) async-start(), calls=%async_computation.8 | async-start | bytes 6291456 | tf_op jit(solution)/shard_map/psum | solution.py:298
  812.6 90.6 %copy-start.7 = (f32[1,524288]{1,0:T(1,128)S(1)}, f32[1,524288]{1,0:T(1,128)}, u32[]{:S(2)}) copy-start(f32[1,524288]{1,0:T(1,128)} %param.17) | copy-start | bytes 6291460
  908.5 7.4 copy-start.38
  912.1 7.6 copy-start.30
  912.2 7.6 copy-start.31
  (61 other events, 173.8 us)
Sparse Core Ops, SparseCore 0:
  764.7 136.5 all-reduce.10
where the time goes:
time: 962 us; the launch traced here: 949 us
  blocking collectives  226 us (23%)
  waiting for transfers between devices  217 us (23%)
  local copies, waits for them, and re-layouts  179 us (19%)
  matrix products  133 us (14%)
  other arithmetic  115 us (12%)
  between operations  48 us (5%)
  starting transfers between devices  30.6 us (3%)
    psum x1, blocking collectives, per_device(): lax.psum((owned_parts[0], owned_parts[1], owned_parts[2], owned_parts[3],...  133 us
    psum x1, waiting for transfers between devices, per_device(): lax.psum((local_sums[0], local_sums[1], local_sums[2], local_sums[3], loc...  88.7 us
    all_to_all x2, waiting for transfers between devices, block_forward(): lax.all_to_all(per_head, 'seq', split_axis=2, concat_axis=1, tiled=True)  57.1 us
    all_to_all x1, blocking collectives, block_backward(): lax.all_to_all(grad_packed, 'seq', split_axis=1, concat_axis=2, tiled=True)  53.8 us
    unnamed x1, blocking collectives  39.1 us
    unnamed x172, local copies, waits for them, and re-layouts  36.9 us
    all_to_all x1, waiting for transfers between devices, block_backward(): lax.all_to_all(grad_packed, 'seq', split_axis=1, concat_axis=2, tiled=True)  34 us
    convert_element_type x2, other arithmetic, block_forward(): hidden_units = jax.nn.gelu(before, approximate=False).astype(jnp.bfloat16)  30.4 us
  transfers between devices with their start and end apart: 8, of which 8 were waited for; matrix products, arithmetic and copies ran while one was open for 3% of the time, Pallas kernels for 0%

commit v1 on v0

--- a/solution.py
+++ b/solution.py
@@ -3,6 +3,7 @@
 import jax.numpy as jnp
 from jax import lax
 from jax.sharding import PartitionSpec as P
+from jax.lax import all_to_all, axis_size
 
 D = 256
 HEADS = 4
@@ -191,8 +192,11 @@
         tiled=True,
     )
     grad_packed = lax.map(attend_single_back, (packed, log_total, grad_heads))
-    projected_gradient = lax.all_to_all(
-        grad_packed, "seq", split_axis=1, concat_axis=2, tiled=True
+    projected_gradient = jnp.concatenate(
+        all_to_all(
+            jnp.stack(jnp.split(grad_packed, axis_size("seq"), axis=1), axis=0), "seq", 0, 0
+        ),
+        2,
     ).reshape(seq_count, quarter, 3 * features)
     grad_joined = jnp.einsum(
         "tck,tcp->kp", normalized_input, projected_gradient, preferred_element_type=jnp.float32

time: 962 us -> 898 us (0.933)
  local copies, waits for them, and re-layouts: 179 us -> 156 us
  blocking collectives: 226 us -> 203 us
  waiting for transfers between devices: 217 us -> 198 us
    all_to_all x1, blocking collectives: 53.8 us -> 31 us  [block_backward(): all_to_all(jnp.stack(jnp.split(grad_packed, axis_size('seq'), axis=1), ax...]
    all_to_all x1, waiting for transfers between devices: 34 us -> 14.5 us  [block_backward(): all_to_all(jnp.stack(jnp.split(grad_packed, axis_size('seq'), axis=1), ax...]
    all_to_all x4 -> x2, local copies, waits for them, and re-layouts: 15.5 us -> 2.04 us  [block_backward(): all_to_all(jnp.stack(jnp.split(grad_packed, axis_size('seq'), axis=1), ax...]
    while x2 -> x0, local copies, waits for them, and re-layouts: 13.1 us -> none  [block_backward(): grad_packed = lax.map(attend_single_back, (packed, log_total, grad_heads))]
where the time goes in v1:
time: 898 us; the launch traced here: 886 us
  blocking collectives  203 us (23%)
  waiting for transfers between devices  198 us (22%)
  local copies, waits for them, and re-layouts  156 us (17%)
  matrix products  133 us (15%)
  other arithmetic  117 us (13%)
  between operations  48 us (5%)
  starting transfers between devices  30.3 us (3%)
    psum x1, blocking collectives, per_device(): lax.psum((owned_parts[0], owned_parts[1], owned_parts[2], owned_parts[3],...  133 us
    psum x1, waiting for transfers between devices, per_device(): lax.psum((local_sums[0], local_sums[1], local_sums[2], local_sums[3], loc...  88.7 us
    all_to_all x2, waiting for transfers between devices, block_forward(): lax.all_to_all(per_head, 'seq', split_axis=2, concat_axis=1, tiled=True)  57.1 us
    unnamed x1, blocking collectives  39.1 us
    unnamed x172, local copies, waits for them, and re-layouts  37.7 us
    all_to_all x1, blocking collectives, block_backward(): all_to_all(jnp.stack(jnp.split(grad_packed, axis_size('seq'), axis=1), ax...  31 us
    convert_element_type x2, other arithmetic, block_forward(): hidden_units = jax.nn.gelu(before, approximate=False).astype(jnp.bfloat16)  30.3 us
    squeeze x24, local copies, waits for them, and re-layouts, attend_items(): attention_output, log_total = lax.map(attend_single, packed_items)  24.6 us
  transfers between devices with their start and end apart: 8, of which 8 were waited for; matrix products, arithmetic and copies ran while one was open for 3% of the time, Pallas kernels for 0%

profile of v1, /device:TPU:0, one launch (start us, length us, event | category | flops | bytes accessed | tf_op | source)
XLA Modules:
  0.0 886.4 jit_solution(13015171303782707043)
XLA Ops:
  40.8 13.1 %fusion.104 = (f32[262144]{0:T(1024)S(1)}, f32[262144]{0:T(1024)}) fusion(pred[]{:T(512)S(6)} %eq.113, f32[1,524288]{1,0:T(1,128)} %param.17, s32[]{:T(128)S(6)} %select_n.271, s32[]{:T(128)S(6)} %select_n.267, pred[]{:T(512)S(6)} %eq.108), kind=kLoop, calls=%fused_computation.229 | loop fusion | flops 524288 | bytes 4194314 | tf_op jit(solution)/shard_map/jit(_where)/select_n | solution.py:250
  69.9 132.7 %all-reduce.12 = (bf16[256,256]{1,0:T(8,128)(2,1)S(1)}, bf16[256,256]{1,0:T(8,128)(2,1)S(1)}, bf16[256,256]{1,0:T(8,128)(2,1)S(1)}, f32[9,256]{1,0:T(8,128)S(1)}...) all-reduce(f32[256,256]{1,0:T(8,128)} %select_n.261, ...), channel_id=1, replica_groups=mesh['dp'=8,'seq'=4] {'dp'}, use_global_device_ids=true, to_apply=%region_5.6 | all-reduce | flops 788736 | bytes 4737024 | tf_op jit(solution)/shard_map/psum | solution.py:251
  213.7 4.5 all-to-all-start
  218.2 28.5 %all-to-all-done = bf16[6,256,4,192]{1,3,0,2:T(8,128)(2,1)} async-done(((bf16[6,256,4,192]{1,3,0,2:T(8,128)(2,1)}), bf16[6,256,4,192]{1,3,0,2:T(8,128)(2,1)}, u32[]{:S(2)}, u32[]{:S(2)}) %all-to-all-start) | async-done | bytes 2359328 | tf_op jit(solution)/shard_map/all_to_all | solution.py:112
  250.2 18.3 %while.44 = (s32[]{:T(128)}, bf16[6,1024,1,64]{1,3,2,0:T(8,128)(2,1)S(1)}, f32[6,1,1024]{2,1,0:T(1,128)S(1)}, bf16[6,1024,1,192]{1,3,2,0:T(8,128)(2,1)}, s32[]{:T(128)}) while((s32[]{:T(128)}, bf16[6,1024,1,64]{1,3,2,0:T(8,128)(2,1)S(1)}, f32[6,1,1024]{2,1,0:T(1,128)S(1)}, bf16[6,1024,1,192]{1,3,2,0:T(8,128)(2,1)}, s32[]{:T(128)}) %tuple.171), condition=%wide.region_9.10_spmd, body=%wide.region_6.9_spmd.sunk | while | flops 284228608 | bytes 13934665 | solution.py:73
  279.2 11.5 %all-to-all-done.1 = bf16[4,2,49152]{2,1,0:T(2,128)(2,1)S(1)} async-done(((bf16[4,2,49152]{2,1,0:T(2,128)(2,1)}), bf16[4,2,49152]{2,1,0:T(2,128)(2,1)S(1)}, u32[]{:S(2)}, u32[]{:S(2)}) %all-to-all-start.1) | async-done | bytes 786464 | tf_op jit(solution)/shard_map/all_to_all | solution.py:114
  301.0 15.2 %multiply_convert_fusion.3 = (bf16[6,256,1024]{2,1,0:T(8,128)(2,1)S(1)}, f32[6,256,1024]{2,1,0:T(8,128)}) fusion(f32[6,256,1024]{2,1,0:T(8,128)S(1)} %get-tuple-element.350, f32[1024]{0:T(1024)S(1)} %bitcast.522, u8[256,1024]{1,0:T(8,128)(4,1)S(1)} %get-tuple-element.217, u8[256,1024]{1,0:T(8,128)(4,1)S(1)} %get-tuple-element.216), kind=kLoop, calls=%fused_computation.130 | loop fusion | flops 111673344 | bytes 16257024 | tf_op jit(solution)/shard_map/convert_element_type | solution.py:126
  328.4 4.5 all-to-all-start.2
  332.9 28.5 %all-to-all-done.2 = bf16[6,256,4,192]{1,3,0,2:T(8,128)(2,1)} async-done(((bf16[6,256,4,192]{1,3,0,2:T(8,128)(2,1)}), bf16[6,256,4,192]{1,3,0,2:T(8,128)(2,1)}, u32[]{:S(2)}, u32[]{:S(2)}) %all-to-all-start.2) | async-done | bytes 2359328 | tf_op jit(solution)/shard_map/all_to_all | solution.py:112
  365.0 18.3 %while.45 = (s32[]{:T(128)}, bf16[6,1024,1,64]{1,3,2,0:T(8,128)(2,1)S(1)}, f32[6,1,1024]{2,1,0:T(1,128)S(1)}, bf16[6,1024,1,192]{1,3,2,0:T(8,128)(2,1)}, s32[]{:T(128)}) while((s32[]{:T(128)}, bf16[6,1024,1,64]{1,3,2,0:T(8,128)(2,1)S(1)}, f32[6,1,1024]{2,1,0:T(1,128)S(1)}, bf16[6,1024,1,192]{1,3,2,0:T(8,128)(2,1)}, s32[]{:T(128)}) %tuple.173), condition=%wide.region_20.21_spmd, body=%wide.region_17.20_spmd.sunk | while | flops 284228608 | bytes 13934665 | solution.py:73
  395.0 10.4 %all-to-all-done.3 = bf16[4,2,49152]{2,1,0:T(2,128)(2,1)S(1)} async-done(((bf16[4,2,49152]{2,1,0:T(2,128)(2,1)}), bf16[4,2,49152]{2,1,0:T(2,128)(2,1)S(1)}, u32[]{:S(2)}, u32[]{:S(2)}) %all-to-all-start.3) | async-done | bytes 786464 | tf_op jit(solution)/shard_map/all_to_all | solution.py:114
  415.6 15.1 %multiply_convert_fusion.2 = (bf16[6,256,1024]{2,1,0:T(8,128)(2,1)}, f32[6,256,1024]{2,1,0:T(8,128)S(1)}) fusion(f32[6,256,1024]{2,1,0:T(8,128)S(1)} %get-tuple-element.353, f32[1024]{0:T(1024)S(1)} %bitcast.524, u8[256,1024]{1,0:T(8,128)(4,1)S(1)} %get-tuple-element.215, u8[256,1024]{1,0:T(8,128)(4,1)S(1)} %get-tuple-element.214), kind=kLoop, calls=%fused_computation.117 | loop fusion | flops 111673344 | bytes 16257024 | tf_op jit(solution)/shard_map/convert_element_type | solution.py:126
  448.9 11.7 %all-to-all-done.4 = bf16[6,256,4,64]{1,3,0,2:T(8,128)(2,1)} async-done(((bf16[6,256,4,64]{1,3,0,2:T(8,128)(2,1)}), bf16[6,256,4,64]{1,3,0,2:T(8,128)(2,1)}, u32[]{:S(2)}, u32[]{:S(2)}) %all-to-all-start.4) | async-done | bytes 786464 | tf_op jit(solution)/shard_map/all_to_all | solution.py:187
  464.4 52.6 %while.46 = (s32[]{:T(128)}, bf16[6,1024,1,192]{1,3,2,0:T(8,128)(2,1)}, bf16[6,1024,1,192]{1,3,2,0:T(8,128)(2,1)}, f32[6,1,1024]{2,1,0:T(1,128)S(1)}, bf16[6,1024,1,64]{1,3,2,0:T(8,128)(2,1)}, /*index=5*/s32[]{:T(128)}) while((s32[]{:T(128)}, bf16[6,1024,1,192]{1,3,2,0:T(8,128)(2,1)}, bf16[6,1024,1,192]{1,3,2,0:T(8,128)(2,1)}, ...), condition=%wide.region_27.28_spmd, body=%wide.region_25.27_spmd.sunk | while | flops 683080704 | bytes 34362956 | solution.py:194
  519.1 31.0 %all_to_all.112 = bf16[4,6,256,1,192]{2,4,1,3,0:T(8,128)(2,1)S(1)} all-to-all(bf16[4,6,256,1,192]{2,4,1,3,0:T(8,128)(2,1)S(1)} %pad_maximum_fusion), channel_id=1, replica_groups=mesh['dp'=8,'seq'=4] {'seq'}, dimensions={0} | all-to-all | bytes 4718592 | tf_op jit(solution)/shard_map/all_to_all | solution.py:196
  560.6 7.0 convert_reduce_fusion
  579.2 4.6 all-to-all-start.6
  599.3 56.6 %while.47 = (s32[]{:T(128)}, bf16[6,1024,1,192]{1,3,2,0:T(8,128)(2,1)}, bf16[6,1024,1,192]{1,3,2,0:T(8,128)(2,1)}, f32[6,1,1024]{2,1,0:T(1,128)}, bf16[6,1024,1,64]{1,3,2,0:T(8,128)(2,1)}, /*index=5*/s32[]{:T(128)}) while((s32[]{:T(128)}, bf16[6,1024,1,192]{1,3,2,0:T(8,128)(2,1)}, bf16[6,1024,1,192]{1,3,2,0:T(8,128)(2,1)}, ...), condition=%wide.region_34.35_spmd, body=%wide.region_32.34_spmd.sunk | while | flops 683080704 | bytes 34362956 | solution.py:194
  659.4 4.5 all-to-all-start.7
  678.0 14.5 %all-to-all-done.7 = bf16[4,6,256,1,192]{2,4,1,3,0:T(8,128)(2,1)} async-done(((bf16[4,6,256,1,192]{2,4,1,3,0:T(8,128)(2,1)}), bf16[4,6,256,1,192]{2,4,1,3,0:T(8,128)(2,1)}, u32[]{:S(2)}, u32[]{:S(2)}) %all-to-all-start.7) | async-done | bytes 2359328 | tf_op jit(solution)/shard_map/all_to_all | solution.py:196
  702.9 39.1 %all-reduce.5 = (f32[192]{0:T(256)S(1)}, f32[192]{0:T(256)S(1)}, f32[1,2304]{1,0:T(1,128)S(1)}) all-reduce(f32[192]{0:T(256)S(1)} %dynamic-update-slice.1, f32[192]{0:T(256)S(1)} %dynamic-update-slice, f32[1,2304]{1,0:T(1,128)S(1)} %bitcast.527), channel_id=3, replica_groups=mesh['dp'=8,'seq'=4] {'dp','seq'}, use_global_device_ids=true, to_apply=%add.4 | all-reduce | flops 2688 | bytes 21504
  749.7 88.7 %all-reduce.11.cloned.1.call-done = (f32[256,4,3,64]{0,3,2,1:T(8,128)}, f32[1,65536]{1,0:T(1,128)}, f32[1,262144]{1,0:T(1,128)}, f32[1,262144]{1,0:T(1,128)}) async-done(((f32[256,4,3,64]{0,3,2,1:T(8,128)}, f32[1,65536]{1,0:T(1,128)}, f32[1,262144]{1,0:T(1,128)}, f32[1,262144]{1,0:T(1,128)}), (f32[256,4,3,64]{0,3,2,1:T(8,128)}, f32[1,65536]{1,0:T(1,128)}, f32[1,262144]{1,0:T(1,128)}, ...) | async-done | bytes 3145744 | tf_op jit(solution)/shard_map/psum | solution.py:302
  862.1 7.1 fusion.103
  869.2 7.1 fusion.107
  (493 shorter events, 358.3 us)
Async XLA Ops:
  69.9 133.1 %copy-start.42 = (bf16[6,256,256]{2,1,0:T(8,128)(2,1)S(1)}, bf16[6,256,256]{2,1,0:T(8,128)(2,1)}, u32[]{:S(2)}) copy-start(bf16[6,256,256]{2,1,0:T(8,128)(2,1)} %param.14) | copy-start | bytes 2359300
  203.0 115.5 %copy-start.35 = (bf16[256,4,3,64]{0,3,2,1:T(8,128)(2,1)}, bf16[256,4,3,64]{0,3,2,1:T(8,128)(2,1)S(1)}, u32[]{:S(2)}) copy-start(bf16[256,4,3,64]{0,3,2,1:T(8,128)(2,1)S(1)} %copy.283) | copy-start | bytes 1179652
  203.0 113.2 %copy-start.63 = (f32[1,256]{1,0:T(1,128)}, f32[1,256]{1,0:T(1,128)S(1)}, u32[]{:S(2)}) copy-start(f32[1,256]{1,0:T(1,128)S(1)} %get-tuple-element.336) | copy-start | bytes 3076
  203.0 115.4 %copy-start.65 = (f32[1,256]{1,0:T(1,128)}, f32[1,256]{1,0:T(1,128)S(1)}, u32[]{:S(2)}) copy-start(f32[1,256]{1,0:T(1,128)S(1)} %get-tuple-element.339) | copy-start | bytes 3076
  203.1 209.2 %copy-start.67 = (f32[1,256]{1,0:T(1,128)}, f32[1,256]{1,0:T(1,128)S(1)}, u32[]{:S(2)}) copy-start(f32[1,256]{1,0:T(1,128)S(1)} %get-tuple-element.337) | copy-start | bytes 3076
  203.3 112.9 %copy-start = (bf16[6,256,256]{1,2,0:T(8,128)(2,1)}, bf16[6,256,256]{1,2,0:T(8,128)(2,1)S(1)}, u32[]{:S(2)}) copy-start(bf16[6,256,256]{1,2,0:T(8,128)(2,1)S(1)} %copy.279) | copy-start | bytes 2359300
  213.7 33.0 %all-to-all-start = ((bf16[6,256,4,192]{1,3,0,2:T(8,128)(2,1)}), bf16[6,256,4,192]{1,3,0,2:T(8,128)(2,1)}, u32[]{:S(2)}, u32[]{:S(2)}) async-start(bf16[6,256,4,192]{1,3,0,2:T(8,128)(2,1)} %copy.287), calls=%async_computation | async-start | bytes 4718592 | tf_op jit(solution)/shard_map/all_to_all | solution.py:112
  275.3 15.5 %all-to-all-start.1 = ((bf16[4,2,49152]{2,1,0:T(2,128)(2,1)}), bf16[4,2,49152]{2,1,0:T(2,128)(2,1)S(1)}, u32[]{:S(2)}, u32[]{:S(2)}) async-start(bf16[4,2,49152]{2,1,0:T(2,128)(2,1)} %reshape.837), calls=%async_computation.1 | async-start | bytes 1572864 | tf_op jit(solution)/shard_map/all_to_all | solution.py:114
  297.4 18.9 %copy-start.3 = (f32[6,256,256]{1,2,0:T(8,128)}, f32[6,256,256]{1,2,0:T(8,128)S(1)}, u32[]{:S(2)}) copy-start(f32[6,256,256]{1,2,0:T(8,128)S(1)} %get-tuple-element.349) | copy-start | bytes 4718596
  301.0 15.3 %copy-start.29 = (f32[6,256,1024]{2,1,0:T(8,128)}, f32[6,256,1024]{2,1,0:T(8,128)S(1)}, u32[]{:S(2)}) copy-start(f32[6,256,1024]{2,1,0:T(8,128)S(1)} %get-tuple-element.350) | copy-start | bytes 18874372
  301.0 15.3 %copy-start.46 = (bf16[1024,256]{0,1:T(8,128)(2,1)S(1)}, bf16[1024,256]{0,1:T(8,128)(2,1)}, u32[]{:S(2)}) copy-start(bf16[1024,256]{0,1:T(8,128)(2,1)} %get-tuple-element.281) | copy-start | bytes 1572868
  328.4 33.0 %all-to-all-start.2 = ((bf16[6,256,4,192]{1,3,0,2:T(8,128)(2,1)}), bf16[6,256,4,192]{1,3,0,2:T(8,128)(2,1)}, u32[]{:S(2)}, u32[]{:S(2)}) async-start(bf16[6,256,4,192]{1,3,0,2:T(8,128)(2,1)} %copy.300), calls=%async_computation.2 | async-start | bytes 4718592 | tf_op jit(solution)/shard_map/all_to_all | solution.py:112
  390.2 15.2 %all-to-all-start.3 = ((bf16[4,2,49152]{2,1,0:T(2,128)(2,1)}), bf16[4,2,49152]{2,1,0:T(2,128)(2,1)S(1)}, u32[]{:S(2)}, u32[]{:S(2)}) async-start(bf16[4,2,49152]{2,1,0:T(2,128)(2,1)} %reshape.839), calls=%async_computation.3 | async-start | bytes 1572864 | tf_op jit(solution)/shard_map/all_to_all | solution.py:114
  415.5 15.1 %copy-start.44 = (bf16[6,256,256]{2,1,0:T(8,128)(2,1)S(1)}, bf16[6,256,256]{2,1,0:T(8,128)(2,1)}, u32[]{:S(2)}) copy-start(bf16[6,256,256]{2,1,0:T(8,128)(2,1)} %param.15) | copy-start | bytes 2359300
  415.6 15.1 %copy-start.47 = (bf16[1024,256]{0,1:T(8,128)(2,1)S(1)}, bf16[1024,256]{0,1:T(8,128)(2,1)}, u32[]{:S(2)}) copy-start(bf16[1024,256]{0,1:T(8,128)(2,1)} %get-tuple-element.281) | copy-start | bytes 1572868
  444.5 16.1 %all-to-all-start.4 = ((bf16[6,256,4,64]{1,3,0,2:T(8,128)(2,1)}), bf16[6,256,4,64]{1,3,0,2:T(8,128)(2,1)}, u32[]{:S(2)}, u32[]{:S(2)}) async-start(bf16[6,256,4,64]{1,3,0,2:T(8,128)(2,1)} %copy.315), calls=%async_computation.4 | async-start | bytes 1572864 | tf_op jit(solution)/shard_map/all_to_all | solution.py:187
  579.2 16.3 %all-to-all-start.6 = ((bf16[6,256,4,64]{1,3,0,2:T(8,128)(2,1)}), bf16[6,256,4,64]{1,3,0,2:T(8,128)(2,1)}, u32[]{:S(2)}, u32[]{:S(2)}) async-start(bf16[6,256,4,64]{1,3,0,2:T(8,128)(2,1)} %copy.332), calls=%async_computation.6 | async-start | bytes 1572864 | tf_op jit(solution)/shard_map/all_to_all | solution.py:187
  659.4 33.1 %all-to-all-start.7 = ((bf16[4,6,256,1,192]{2,4,1,3,0:T(8,128)(2,1)}), bf16[4,6,256,1,192]{2,4,1,3,0:T(8,128)(2,1)}, u32[]{:S(2)}, u32[]{:S(2)}) async-start(bf16[4,6,256,1,192]{2,4,1,3,0:T(8,128)(2,1)} %pad_maximum_fusion.1), calls=%async_computation.7 | async-start | bytes 4718592 | tf_op jit(solution)/shard_map/all_to_all | solution.py:196
  664.0 174.4 %all-reduce.11.cloned.1.call-start = ((), (), s32[]{:S(2)}) async-start(), calls=%async_computation.8 | async-start | bytes 6291456 | tf_op jit(solution)/shard_map/psum | solution.py:302
  678.0 16.4 %copy-start.1 = (bf16[6,256,256]{1,2,0:T(8,128)(2,1)S(1)}, bf16[6,256,256]{1,2,0:T(8,128)(2,1)}, u32[]{:S(2)}) copy-start(bf16[6,256,256]{1,2,0:T(8,128)(2,1)} %copy-done) | copy-start | bytes 2359300
  678.0 16.4 %copy-start.51 = (f32[6,256]{1,0:T(8,128)S(1)}, f32[6,256]{1,0:T(8,128)}, u32[]{:S(2)}) copy-start(f32[6,256]{1,0:T(8,128)} %copy-done.50) | copy-start | bytes 18436
  678.0 16.4 %copy-start.56 = (f32[6,256]{1,0:T(8,128)S(1)}, f32[6,256]{1,0:T(8,128)}, u32[]{:S(2)}) copy-start(f32[6,256]{1,0:T(8,128)} %copy-done.55) | copy-start | bytes 18436
  678.0 16.4 %copy-start.66 = (f32[1,256]{1,0:T(1,128)S(1)}, f32[1,256]{1,0:T(1,128)}, u32[]{:S(2)}) copy-start(f32[1,256]{1,0:T(1,128)} %copy-done.65) | copy-start | bytes 3076
  749.7 90.6 %copy-start.7 = (f32[1,524288]{1,0:T(1,128)S(1)}, f32[1,524288]{1,0:T(1,128)}, u32[]{:S(2)}) copy-start(f32[1,524288]{1,0:T(1,128)} %param.17) | copy-start | bytes 6291460
  (61 other events, 195.4 us)
Sparse Core Ops, SparseCore 0:
  701.7 136.5 all-reduce.10
